TPU v7x, 128 devices: a whole 4x4x4 slice. The times are simulated.
128 devices in a mesh: seq: 32 (over z, x, core), group: 4 (over y).
Axes of the slice: x: 4, y: 4, z: 4, core: 2. Of those that a mesh axis runs over, the one named last changes fastest.
Arguments:
- new_queries: bfloat16 [32, 8, 8, 128], P('seq', 'group'), may hold values from -6 to 6
- stored_keys: bfloat16 [32, 8, 16384, 128], P(None, 'group', 'seq'), may hold values from -6 to 6
- stored_values: bfloat16 [32, 8, 16384, 128], P(None, 'group', 'seq'), may hold values from -6 to 6
- used_length: int32 [32], replicated, may hold values from 8192 to 16384
- out_weight: bfloat16 [8, 8, 128, 5120], P('group'), may hold values from -0.0625 to 0.0625
Outputs:
- token_out: bfloat16 [32, 5120], P('seq', 'group')
All inputs are finite; a program needn't handle non-finite values.
Results may differ from a plain program's by a relative error of at most 0.0025.
Values may be sent and summed in bfloat16 or wider, within the bound.
No kernel may reach another device: no remote copies, remote signals or barrier semaphores. Data moves between devices by JAX's collectives and lax.ppermute only.
A program may use at most 128 MiB of HBM per device.

v0:
```python
import jax
import jax.numpy as jnp
from jax import lax
from jax.sharding import PartitionSpec as P

HEAD_SIZE = 128


def per_device(new_queries, stored_keys, stored_values, used_length, out_weight):
    all_queries = lax.all_gather(new_queries, "seq", axis=0, tiled=True)
    logit = jnp.einsum(
        "bkgd,bktd->bkgt", all_queries, stored_keys, preferred_element_type=jnp.float32
    ) * HEAD_SIZE ** (-0.5)
    positions = lax.axis_index("seq") * stored_keys.shape[2] + jnp.arange(stored_keys.shape[2])
    filled = positions[None, :] < used_length[:, None]
    logit = jnp.where(filled[:, None, None, :], logit, -1e30)
    top = jnp.max(logit, axis=-1)
    part = jnp.where(filled[:, None, None, :], jnp.exp(logit - top[..., None]), 0.0)
    weight_sum = jnp.sum(part, axis=-1)
    read_sum = jnp.einsum(
        "bkgt,bktd->bkgd", part, stored_values.astype(jnp.float32), precision=lax.Precision.HIGHEST
    )
    tops, sums, parts = (
        lax.all_to_all(top[None], "seq", split_axis=1, concat_axis=0, tiled=True),
        lax.all_to_all(weight_sum[None], "seq", split_axis=1, concat_axis=0, tiled=True),
        lax.all_to_all(read_sum[None], "seq", split_axis=1, concat_axis=0, tiled=True),
    )
    best = jnp.max(tops, axis=0)
    scale = jnp.exp(tops - best)
    weight_own = jnp.sum(sums * scale, axis=0)
    read_own = jnp.sum(parts * scale[..., None], axis=0)
    read = (read_own / weight_own[..., None]).astype(jnp.bfloat16)
    term = jnp.einsum("bkgd,kgdm->bm", read, out_weight, preferred_element_type=jnp.float32)
    token_out = lax.psum_scatter(term, "group", scatter_dimension=1, tiled=True).astype(
        jnp.bfloat16
    )
    return token_out


def solution(mesh):
    in_specs = (
        P("seq", "group", None, None),
        P(None, "group", "seq", None),
        P(None, "group", "seq", None),
        P(),
        P("group", None, None, None),
    )
    out_specs = P("seq", "group")
    return jax.shard_map(
        per_device, mesh=mesh, in_specs=in_specs, out_specs=out_specs, check_vma=False
    )
```

profile of v0, /device:TPU:1, one launch (start us, length us, event | category | flops | bytes accessed | tf_op | source)
XLA Modules:
  0.0 134.0 jit_solution(4825849419178507323)
XLA Ops:
  6.5 27.3 %all_gather.3 = bf16[32,2,8,128]{3,2,1,0:T(8,128)(2,1)S(1)} all-gather(bf16[1,2,8,128]{3,2,1,0:T(8,128)(2,1)} %param.5), channel_id=1, replica_groups=mesh['seq'=32,'group'=4] {'seq'}, dimensions={0}, use_global_device_ids=true | all-gather | bytes 135168 | tf_op jit(solution)/shard_map/all_gather | solution.py:10
  33.9 0.7 broadcast_compare_fusion
  34.6 6.4 %fusion.18 = (f32[32,2,8]{2,1,0:T(2,128)}, f32[32,2,8,512]{3,2,1,0:T(8,128)S(1)}) fusion(bf16[32,2,8,128]{3,2,1,0:T(8,128)(2,1)S(1)} %all_gather.3, bf16[32,2,512,128]{3,2,1,0:T(8,128)(2,1)} %param.6, pred[32,512]{1,0:T(8,128)(4,1)S(1)} %broadcast_compare_fusion), kind=kOutput, calls=%fused_computation.25 | convolution fusion | flops 67894784 | bytes 9586688 | tf_op jit(solution)/shard_map/bkgd,bktd->bkgt/dot_general | solution.py:11
  41.0 4.9 %all-to-all-start.1 = ((f32[1,32,2,8]{3,2,0,1:T(2,128)}), f32[1,32,2,8]{3,2,0,1:T(2,128)S(1)}, u32[]{:S(2)}, u32[]{:S(2)}) async-start(f32[1,32,2,8]{3,2,0,1:T(2,128)} %bitcast.3), calls=%async_computation.1 | async-start | bytes 65536 | tf_op jit(solution)/shard_map/all_to_all | solution.py:24
  45.9 1.8 %fusion.6 = f32[32,2,8]{2,1,0:T(2,128)} fusion(f32[32,2,8,512]{3,2,1,0:T(8,128)S(1)} %get-tuple-element.6, f32[32,2,8]{2,1,0:T(2,128)} %get-tuple-element.5, pred[32,512]{1,0:T(8,128)(4,1)S(1)} %broadcast_compare_fusion), kind=kLoop, calls=%fused_computation.7 | loop fusion | flops 785920 | bytes 1069056 | tf_op jit(solution)/shard_map/reduce_sum | solution.py:19
  47.6 5.5 %all-to-all-done.1 = f32[1,32,2,8]{3,2,0,1:T(2,128)S(1)} async-done(((f32[1,32,2,8]{3,2,0,1:T(2,128)}), f32[1,32,2,8]{3,2,0,1:T(2,128)S(1)}, u32[]{:S(2)}, u32[]{:S(2)}) %all-to-all-start.1) | async-done | bytes 2080 | tf_op jit(solution)/shard_map/all_to_all | solution.py:24
  53.1 3.9 %all-to-all-start.2 = ((f32[1,32,2,8]{3,2,0,1:T(2,128)}), f32[1,32,2,8]{3,2,0,1:T(2,128)S(1)}, u32[]{:S(2)}, u32[]{:S(2)}) async-start(f32[1,32,2,8]{3,2,0,1:T(2,128)} %bitcast.5), calls=%async_computation.2 | async-start | bytes 65536 | tf_op jit(solution)/shard_map/all_to_all | solution.py:25
  57.0 6.5 %convolution_bitcast_fusion = f32[1,32,2,8,128]{4,3,2,0,1:T(8,128)} fusion(bf16[32,2,512,128]{3,2,1,0:T(8,128)(2,1)} %param.7, f32[32,2,8,512]{3,2,1,0:T(8,128)S(1)} %get-tuple-element.6, f32[32,2,8]{2,1,0:T(2,128)} %get-tuple-element.5, pred[32,512]{1,0:T(8,128)(4,1)S(1)} %broadcast_compare_fusion), kind=kOutput, calls=%fused_computation.5 | convolution fusion | flops 403177472 | bytes 9717760 | tf_op jit(solution)/shard_map/bkgt,bktd->bkgd/dot_general | solution.py:20
  63.6 0.8 all-to-all-done.2
  64.4 6.7 %all-to-all-start = ((f32[1,32,2,8,128]{4,3,2,0,1:T(8,128)}), f32[1,32,2,8,128]{4,3,2,0,1:T(8,128)S(1)}, u32[]{:S(2)}, u32[]{:S(2)}) async-start(f32[1,32,2,8,128]{4,3,2,0,1:T(8,128)} %convolution_bitcast_fusion), calls=%async_computation | async-start | bytes 524288 | tf_op jit(solution)/shard_map/all_to_all | solution.py:26
  71.1 0.0 reduce-scatter.4.cloned.1.call-start
  71.1 0.1 fusion.14
  71.2 8.7 %all-to-all-done = f32[1,32,2,8,128]{4,3,2,0,1:T(8,128)S(1)} async-done(((f32[1,32,2,8,128]{4,3,2,0,1:T(8,128)}), f32[1,32,2,8,128]{4,3,2,0,1:T(8,128)S(1)}, u32[]{:S(2)}, u32[]{:S(2)}) %all-to-all-start) | async-done | bytes 262176 | tf_op jit(solution)/shard_map/all_to_all | solution.py:26
  80.0 0.1 fusion.10
  80.1 0.1 fusion.16
  80.2 13.4 %fusion.2 = f32[5120,1]{1,0:T(8,128)} fusion(bf16[2,8,128,5120]{3,2,1,0:T(8,128)(2,1)} %param.9, bf16[2,8,128,1]{2,1,0,3:T(8,128)(2,1)S(1)} %fusion.16), kind=kOutput, calls=%fused_computation.2 | convolution fusion | flops 20971520 | bytes 20996096 | tf_op jit(solution)/shard_map/bkgd,kgdm->bm/dot_general | solution.py:33
  93.6 0.0 reduce-scatter.4.cloned.1.call-update
  93.6 31.6 %reduce-scatter.4.cloned.1.call-done = f32[1280,1]{1,0:T(8,128)} async-done(((f32[5120,1]{1,0:T(8,128)}), f32[1280,1]{1,0:T(8,128)}) %reduce-scatter.4.cloned.1.call-update) | async-done | bytes 5136
  125.3 1.9 %copy.11 = bf16[1,1280]{1,0:T(2,128)(2,1)} copy(f32[1,1280]{0,1:T(8,128)} %bitcast.41) | data formatting | bytes 7680
  (3 shorter events, 0.1 us)
Async XLA Ops:
  41.0 12.2 %all-to-all-start.1 = ((f32[1,32,2,8]{3,2,0,1:T(2,128)}), f32[1,32,2,8]{3,2,0,1:T(2,128)S(1)}, u32[]{:S(2)}, u32[]{:S(2)}) async-start(f32[1,32,2,8]{3,2,0,1:T(2,128)} %bitcast.3), calls=%async_computation.1 | async-start | bytes 65536 | tf_op jit(solution)/shard_map/all_to_all | solution.py:24
  53.1 11.3 %all-to-all-start.2 = ((f32[1,32,2,8]{3,2,0,1:T(2,128)}), f32[1,32,2,8]{3,2,0,1:T(2,128)S(1)}, u32[]{:S(2)}, u32[]{:S(2)}) async-start(f32[1,32,2,8]{3,2,0,1:T(2,128)} %bitcast.5), calls=%async_computation.2 | async-start | bytes 65536 | tf_op jit(solution)/shard_map/all_to_all | solution.py:25
  64.4 15.6 %all-to-all-start = ((f32[1,32,2,8,128]{4,3,2,0,1:T(8,128)}), f32[1,32,2,8,128]{4,3,2,0,1:T(8,128)S(1)}, u32[]{:S(2)}, u32[]{:S(2)}) async-start(f32[1,32,2,8,128]{4,3,2,0,1:T(8,128)} %convolution_bitcast_fusion), calls=%async_computation | async-start | bytes 524288 | tf_op jit(solution)/shard_map/all_to_all | solution.py:26
  71.1 54.2 %reduce-scatter.4.cloned.1.call-start = ((), (), s32[]{:S(2)}) async-start(), calls=%async_computation.4 | async-start | bytes 3276800
Sparse Core Ops, SparseCore 0:
  93.8 31.4 reduce-scatter.3
where the time goes:
time: 135 us; the launch traced here: 134 us
  waiting for transfers between devices  46.7 us (35%)
  blocking collectives  27.3 us (20%)
  matrix products  26.3 us (19%)
  starting transfers between devices  15.5 us (11%)
  between operations  13.4 us (10%)
  other arithmetic  2.83 us (2%)
  local copies, waits for them, and re-layouts  1.91 us (1%)
    unnamed x2, waiting for transfers between devices  31.6 us
    all_gather x1, blocking collectives, per_device(): all_queries = lax.all_gather(new_queries, 'seq', axis=0, tiled=True)  27.3 us
    dot_general x1, matrix products, per_device(): jnp.einsum('bkgd,kgdm->bm', read, out_weight, preferred_element_type=jnp....  13.4 us
    all_to_all x1, waiting for transfers between devices, per_device(): lax.all_to_all(read_sum[None], 'seq', split_axis=1, concat_axis=0, tiled=...  8.74 us
    all_to_all x1, starting transfers between devices, per_device(): lax.all_to_all(read_sum[None], 'seq', split_axis=1, concat_axis=0, tiled=...  6.68 us
    dot_general x1, matrix products, per_device(): jnp.einsum('bkgt,bktd->bkgd', part, stored_values.astype(jnp.float32), pr...  6.5 us
    dot_general x1, matrix products, per_device(): jnp.einsum('bkgd,bktd->bkgt', all_queries, stored_keys, preferred_element...  6.36 us
    all_to_all x1, waiting for transfers between devices, per_device(): lax.all_to_all(top[None], 'seq', split_axis=1, concat_axis=0, tiled=True)  5.49 us
  transfers between devices with their start and end apart: 4, of which 4 were waited for; matrix products, arithmetic and copies ran while one was open for 6% of the time, Pallas kernels for 0%

commit v1 on v0

--- a/solution.py
+++ b/solution.py
@@ -7,7 +7,12 @@
 
 
 def per_device(new_queries, stored_keys, stored_values, used_length, out_weight):
-    all_queries = lax.all_gather(new_queries, "seq", axis=0, tiled=True)
+
+    def group_do(here_x):
+        prior = jnp.concatenate([here_x] * lax.axis_size("seq"), axis=0)
+        return lax.all_to_all(prior, "seq", 0, 0, tiled=True)
+
+    all_queries = group_do(new_queries)
     logit = jnp.einsum(
         "bkgd,bktd->bkgt", all_queries, stored_keys, preferred_element_type=jnp.float32
     ) * HEAD_SIZE ** (-0.5)

time: 135 us -> 124 us (0.919)
  blocking collectives: 27.3 us -> 0 us
  starting transfers between devices: 15.5 us -> 23.9 us
  waiting for transfers between devices: 46.7 us -> 53.7 us
    all_gather x1 -> x0, blocking collectives: 27.3 us -> none  [per_device(): all_queries = lax.all_gather(new_queries, 'seq', axis=0, tiled=True)]
    all_to_all x0 -> x1, starting transfers between devices: none -> 9.42 us  [group_do(): return lax.all_to_all(prior, 'seq', 0, 0, tiled=True)]
    all_to_all x0 -> x1, waiting for transfers between devices: none -> 6.84 us  [group_do(): return lax.all_to_all(prior, 'seq', 0, 0, tiled=True)]
  transfers between devices with their start and end apart: 4 -> 5, of which waited for: 4 -> 5; matrix products, arithmetic and copies ran while one was open for 6% -> 7% of each run, Pallas kernels for 0% -> 0%
where the time goes in v1:
time: 124 us; the launch traced here: 123 us
  waiting for transfers between devices  53.7 us (43%)
  matrix products  26.3 us (21%)
  starting transfers between devices  23.9 us (19%)
  between operations  13.5 us (11%)
  local copies, waits for them, and re-layouts  3.25 us (3%)
  other arithmetic  2.84 us (2%)
    unnamed x2, waiting for transfers between devices  31.6 us
    dot_general x1, matrix products, per_device(): jnp.einsum('bkgd,kgdm->bm', read, out_weight, preferred_element_type=jnp....  13.4 us
    all_to_all x1, starting transfers between devices, group_do(): return lax.all_to_all(prior, 'seq', 0, 0, tiled=True)  9.42 us
    all_to_all x1, waiting for transfers between devices, per_device(): lax.all_to_all(read_sum[None], 'seq', split_axis=1, concat_axis=0, tiled=...  8.74 us
    all_to_all x1, waiting for transfers between devices, group_do(): return lax.all_to_all(prior, 'seq', 0, 0, tiled=True)  6.84 us
    all_to_all x1, starting transfers between devices, per_device(): lax.all_to_all(read_sum[None], 'seq', split_axis=1, concat_axis=0, tiled=...  6.69 us
    dot_general x1, matrix products, per_device(): jnp.einsum('bkgt,bktd->bkgd', part, stored_values.astype(jnp.float32), pr...  6.5 us
    dot_general x1, matrix products, per_device(): jnp.einsum('bkgd,bktd->bkgt', all_queries, stored_keys, preferred_element...  6.36 us
  transfers between devices with their start and end apart: 5, of which 5 were waited for; matrix products, arithmetic and copies ran while one was open for 7% of the time, Pallas kernels for 0%

profile of v1, /device:TPU:1, one launch (start us, length us, event | category | flops | bytes accessed | tf_op | source)
XLA Modules:
  0.0 123.4 jit_solution(7740491030624859670)
XLA Ops:
  6.5 1.3 %concatenate.3 = bf16[32,2,8,128]{3,2,1,0:T(8,128)(2,1)} broadcast(bf16[2,8,128]{2,1,0:T(8,128)(2,1)} %bitcast.43), dimensions={1,2,3} | broadcast | bytes 135168 | tf_op jit(solution)/shard_map/concatenate | solution.py:12
  7.9 9.4 %all-to-all-start = ((bf16[32,2,8,128]{3,2,1,0:T(8,128)(2,1)}), bf16[32,2,8,128]{3,2,1,0:T(8,128)(2,1)S(1)}, u32[]{:S(2)}, u32[]{:S(2)}) async-start(bf16[32,2,8,128]{3,2,1,0:T(8,128)(2,1)} %concatenate.3), calls=%async_computation | async-start | bytes 262144 | tf_op jit(solution)/shard_map/all_to_all | solution.py:13
  17.3 0.7 broadcast_compare_fusion
  18.1 6.8 %all-to-all-done = bf16[32,2,8,128]{3,2,1,0:T(8,128)(2,1)S(1)} async-done(((bf16[32,2,8,128]{3,2,1,0:T(8,128)(2,1)}), bf16[32,2,8,128]{3,2,1,0:T(8,128)(2,1)S(1)}, u32[]{:S(2)}, u32[]{:S(2)}) %all-to-all-start) | async-done | bytes 131104 | tf_op jit(solution)/shard_map/all_to_all | solution.py:13
  24.9 6.4 %fusion.18 = (f32[32,2,8]{2,1,0:T(2,128)}, f32[32,2,8,512]{3,2,1,0:T(8,128)S(1)}) fusion(bf16[32,2,8,128]{3,2,1,0:T(8,128)(2,1)S(1)} %all-to-all-done, bf16[32,2,512,128]{3,2,1,0:T(8,128)(2,1)} %param.6, pred[32,512]{1,0:T(8,128)(4,1)S(1)} %broadcast_compare_fusion), kind=kOutput, calls=%fused_computation.25 | convolution fusion | flops 67894784 | bytes 9586688 | tf_op jit(solution)/shard_map/bkgd,bktd->bkgt/dot_general | solution.py:16
  31.3 3.9 %all-to-all-start.2 = ((f32[1,32,2,8]{3,2,0,1:T(2,128)}), f32[1,32,2,8]{3,2,0,1:T(2,128)S(1)}, u32[]{:S(2)}, u32[]{:S(2)}) async-start(f32[1,32,2,8]{3,2,0,1:T(2,128)} %bitcast.4), calls=%async_computation.2 | async-start | bytes 65536 | tf_op jit(solution)/shard_map/all_to_all | solution.py:29
  35.2 1.8 %fusion.6 = f32[32,2,8]{2,1,0:T(2,128)} fusion(f32[32,2,8,512]{3,2,1,0:T(8,128)S(1)} %get-tuple-element.6, f32[32,2,8]{2,1,0:T(2,128)} %get-tuple-element.5, pred[32,512]{1,0:T(8,128)(4,1)S(1)} %broadcast_compare_fusion), kind=kLoop, calls=%fused_computation.7 | loop fusion | flops 785920 | bytes 1069056 | tf_op jit(solution)/shard_map/reduce_sum | solution.py:24
  36.9 5.6 %all-to-all-done.2 = f32[1,32,2,8]{3,2,0,1:T(2,128)S(1)} async-done(((f32[1,32,2,8]{3,2,0,1:T(2,128)}), f32[1,32,2,8]{3,2,0,1:T(2,128)S(1)}, u32[]{:S(2)}, u32[]{:S(2)}) %all-to-all-start.2) | async-done | bytes 2080 | tf_op jit(solution)/shard_map/all_to_all | solution.py:29
  42.5 3.9 %all-to-all-start.3 = ((f32[1,32,2,8]{3,2,0,1:T(2,128)}), f32[1,32,2,8]{3,2,0,1:T(2,128)S(1)}, u32[]{:S(2)}, u32[]{:S(2)}) async-start(f32[1,32,2,8]{3,2,0,1:T(2,128)} %bitcast.6), calls=%async_computation.3 | async-start | bytes 65536 | tf_op jit(solution)/shard_map/all_to_all | solution.py:30
  46.4 6.5 %convolution_bitcast_fusion = f32[1,32,2,8,128]{4,3,2,0,1:T(8,128)} fusion(bf16[32,2,512,128]{3,2,1,0:T(8,128)(2,1)} %param.7, f32[32,2,8,512]{3,2,1,0:T(8,128)S(1)} %get-tuple-element.6, f32[32,2,8]{2,1,0:T(2,128)} %get-tuple-element.5, pred[32,512]{1,0:T(8,128)(4,1)S(1)} %broadcast_compare_fusion), kind=kOutput, calls=%fused_computation.5 | convolution fusion | flops 403177472 | bytes 9717760 | tf_op jit(solution)/shard_map/bkgt,bktd->bkgd/dot_general | solution.py:25
  53.0 0.8 all-to-all-done.3
  53.8 6.7 %all-to-all-start.1 = ((f32[1,32,2,8,128]{4,3,2,0,1:T(8,128)}), f32[1,32,2,8,128]{4,3,2,0,1:T(8,128)S(1)}, u32[]{:S(2)}, u32[]{:S(2)}) async-start(f32[1,32,2,8,128]{4,3,2,0,1:T(8,128)} %convolution_bitcast_fusion), calls=%async_computation.1 | async-start | bytes 524288 | tf_op jit(solution)/shard_map/all_to_all | solution.py:31
  60.5 0.0 reduce-scatter.4.cloned.1.call-start
  60.5 0.1 fusion.14
  60.6 8.7 %all-to-all-done.1 = f32[1,32,2,8,128]{4,3,2,0,1:T(8,128)S(1)} async-done(((f32[1,32,2,8,128]{4,3,2,0,1:T(8,128)}), f32[1,32,2,8,128]{4,3,2,0,1:T(8,128)S(1)}, u32[]{:S(2)}, u32[]{:S(2)}) %all-to-all-start.1) | async-done | bytes 262176 | tf_op jit(solution)/shard_map/all_to_all | solution.py:31
  69.4 0.1 fusion.10
  69.5 0.1 fusion.16
  69.6 13.4 %fusion.2 = f32[5120,1]{1,0:T(8,128)} fusion(bf16[2,8,128,5120]{3,2,1,0:T(8,128)(2,1)} %param.9, bf16[2,8,128,1]{2,1,0,3:T(8,128)(2,1)S(1)} %fusion.16), kind=kOutput, calls=%fused_computation.2 | convolution fusion | flops 20971520 | bytes 20996096 | tf_op jit(solution)/shard_map/bkgd,kgdm->bm/dot_general | solution.py:38
  83.0 0.0 reduce-scatter.4.cloned.1.call-update
  83.0 31.6 %reduce-scatter.4.cloned.1.call-done = f32[1280,1]{1,0:T(8,128)} async-done(((f32[5120,1]{1,0:T(8,128)}), f32[1280,1]{1,0:T(8,128)}) %reduce-scatter.4.cloned.1.call-update) | async-done | bytes 5136
  114.7 1.9 %copy.11 = bf16[1,1280]{1,0:T(2,128)(2,1)} copy(f32[1,1280]{0,1:T(8,128)} %bitcast.42) | data formatting | bytes 7680
  (3 shorter events, 0.1 us)
Async XLA Ops:
  7.9 17.0 %all-to-all-start = ((bf16[32,2,8,128]{3,2,1,0:T(8,128)(2,1)}), bf16[32,2,8,128]{3,2,1,0:T(8,128)(2,1)S(1)}, u32[]{:S(2)}, u32[]{:S(2)}) async-start(bf16[32,2,8,128]{3,2,1,0:T(8,128)(2,1)} %concatenate.3), calls=%async_computation | async-start | bytes 262144 | tf_op jit(solution)/shard_map/all_to_all | solution.py:13
  31.3 11.3 %all-to-all-start.2 = ((f32[1,32,2,8]{3,2,0,1:T(2,128)}), f32[1,32,2,8]{3,2,0,1:T(2,128)S(1)}, u32[]{:S(2)}, u32[]{:S(2)}) async-start(f32[1,32,2,8]{3,2,0,1:T(2,128)} %bitcast.4), calls=%async_computation.2 | async-start | bytes 65536 | tf_op jit(solution)/shard_map/all_to_all | solution.py:29
  42.5 11.3 %all-to-all-start.3 = ((f32[1,32,2,8]{3,2,0,1:T(2,128)}), f32[1,32,2,8]{3,2,0,1:T(2,128)S(1)}, u32[]{:S(2)}, u32[]{:S(2)}) async-start(f32[1,32,2,8]{3,2,0,1:T(2,128)} %bitcast.6), calls=%async_computation.3 | async-start | bytes 65536 | tf_op jit(solution)/shard_map/all_to_all | solution.py:30
  53.8 15.6 %all-to-all-start.1 = ((f32[1,32,2,8,128]{4,3,2,0,1:T(8,128)}), f32[1,32,2,8,128]{4,3,2,0,1:T(8,128)S(1)}, u32[]{:S(2)}, u32[]{:S(2)}) async-start(f32[1,32,2,8,128]{4,3,2,0,1:T(8,128)} %convolution_bitcast_fusion), calls=%async_computation.1 | async-start | bytes 524288 | tf_op jit(solution)/shard_map/all_to_all | solution.py:31
  60.5 54.2 %reduce-scatter.4.cloned.1.call-start = ((), (), s32[]{:S(2)}) async-start(), calls=%async_computation.5 | async-start | bytes 3276800
Sparse Core Ops, SparseCore 0:
  83.2 31.4 reduce-scatter.3
